TPU v7x, 256 devices: a whole 4x4x8 slice. The times are simulated.
256 devices in a mesh: tm: 64 (over z, x, core), blk: 4 (over y).
Axes of the slice: x: 4, y: 4, z: 8, core: 2. Of those that a mesh axis runs over, the one named last changes fastest.
Arguments:
- prior_mean: float32 [512], replicated, may hold values from -6 to 6
- after_mean: float32 [512], replicated, may hold values from -6 to 6
- filter_map: float32 [128, 512, 512], P('tm', 'blk'), may hold values from -1 to 1.5
- smoother_gain: float32 [128, 512, 512], P('tm', 'blk'), may hold values from -1 to 1.5
- smoother_map: float32 [128, 512, 512], P('tm', 'blk'), may hold values from -1 to 1.5
- obs_gain: float32 [128, 512, 128], P('tm', 'blk'), may hold values from -0.5 to 0.5
- observations: float32 [128, 128], P('tm'), may hold values from -6 to 6
Outputs:
- filtered: float32 [128, 512], P('tm', 'blk')
- smoothed: float32 [128, 512], P('tm', 'blk')
All inputs are finite; a program needn't handle non-finite values.
Results may differ from a plain program's by a relative error of at most 0.0003.
Values sent between devices are 32-bit elements; how exact they have to be, the bound alone decides.
A program may use at most 128 MiB of HBM per device.

v0:
```python
import jax
import jax.numpy as jnp
from jax import lax
from jax.sharding import Mesh
from jax.sharding import PartitionSpec as P

TM = ("tm_0", "tm_1", "tm_2")


def neutral_like(value, identity):
    return jax.tree.map(
        lambda part, zero: jnp.zeros_like(part) + jnp.asarray(zero, part.dtype), value, identity
    )


def prefix_by_axis(value, axes, combine, identity, reverse):
    before = start = neutral_like(value, identity)
    so_far = value
    for axis in reversed(axes):
        length, index = (lax.axis_size(axis), lax.axis_index(axis))
        pieces = jax.tree.map(lambda part: lax.all_gather(part, axis), so_far)
        inside, so_far = (start, start)
        for k in reversed(range(length)) if reverse else range(length):
            passed = k > index if reverse else k < index
            so_far = combine(so_far, jax.tree.map(lambda part: part[k], pieces))
            inside = jax.tree.map(lambda new, old: jnp.where(passed, new, old), so_far, inside)
        before = combine(inside, before)
    return before


def chain_combine(earlier, later):
    highest = lax.Precision.HIGHEST
    joined_map = jnp.dot(later[0], earlier[0], precision=highest)
    joined_offset = jnp.dot(later[0], earlier[1], precision=highest) + later[1]
    return (joined_map, joined_offset)


def shards(prior_mean, after_mean, filter_map, smoother_gain, smoother_map, obs_gain, observations):
    highest = lax.Precision.HIGHEST
    steps = filter_map.shape[0]
    rows = filter_map.shape[1]
    width = filter_map.shape[2]
    first_row = lax.axis_index("blk") * rows
    drive_rows = jnp.einsum("tro,to->tr", obs_gain, observations, precision=highest)
    full_filter, full_gain, drive = (
        lax.all_gather(filter_map, "blk", axis=1, tiled=True),
        lax.all_gather(smoother_gain, "blk", axis=1, tiled=True),
        lax.all_gather(drive_rows, "blk", axis=1, tiled=True),
    )
    identity = jnp.eye(width, dtype=jnp.float32)
    nothing = jnp.zeros((width,), jnp.float32)
    offset = nothing
    for index in range(steps):
        offset = jnp.dot(full_filter[index], offset, precision=highest) + drive[index]
    composite = full_filter[steps - 1]
    index = 0
    composite = jnp.dot(composite, full_filter[index], precision=highest)
    total = prefix_by_axis((composite, offset), TM, chain_combine, (identity, nothing), False)
    entering = jnp.dot(total[0], prior_mean, precision=highest) + total[1]
    current = entering
    filtered_list = []
    for index in range(steps):
        current = jnp.dot(full_filter[index], current, precision=highest) + drive[index]
        filtered_list.append(current)
    filtered_full = jnp.stack(filtered_list, axis=0)
    filtered_rows = lax.dynamic_slice_in_dim(filtered_full, first_row, rows, 1)
    pulled_rows = jnp.einsum("trk,tk->tr", smoother_map, filtered_full, precision=highest)
    pulled = lax.all_gather(pulled_rows, "blk", axis=1, tiled=True)
    offset = nothing
    for index in range(steps - 1, -1, -1):
        offset = jnp.dot(full_gain[index], offset, precision=highest) + pulled[index]
    composite = full_gain[0]
    index = 1
    composite = jnp.dot(composite, full_gain[index], precision=highest)
    total = prefix_by_axis((composite, offset), TM, chain_combine, (identity, nothing), True)
    leaving = jnp.dot(total[0], after_mean, precision=highest) + total[1]
    current = leaving
    smoothed_list = []
    for index in range(steps - 1, -1, -1):
        current = jnp.dot(full_gain[index], current, precision=highest) + pulled[index]
        smoothed_list.append(current)
    smoothed_full = jnp.stack(smoothed_list[::-1], axis=0)
    smoothed_rows = lax.dynamic_slice_in_dim(smoothed_full, first_row, rows, 1)
    return (filtered_rows, smoothed_rows)


def solution(mesh):
    torus = Mesh(mesh.devices.reshape(8, 4, 2, mesh.shape["blk"]), ("tm_0", "tm_1", "tm_2", "blk"))
    in_specs = (
        P(),
        P(),
        P(TM, "blk", None),
        P(TM, "blk", None),
        P(TM, "blk", None),
        P(TM, "blk", None),
        P(TM, None),
    )
    out_specs = (P(TM, "blk"), P(TM, "blk"))
    return jax.shard_map(
        shards, mesh=torus, in_specs=in_specs, out_specs=out_specs, check_vma=False
    )
```

profile of v0, /device:TPU:1, one launch (start us, length us, event | category | flops | bytes accessed | tf_op | source)
XLA Modules:
  0.0 462.8 jit_solution(7283257458123513231)
XLA Ops:
  8.7 38.1 %all-gather.27.cloned.1.call-done = f32[2,512,512]{2,1,0:T(8,128)} async-done(((f32[2,128,512]{2,1,0:T(8,128)}), f32[2,512,512]{2,1,0:T(8,128)}) %all-gather.27.cloned.1.call-update) | async-done | bytes 2097168 | tf_op jit(solution)/shard_map/all_gather | solution.py:46
  46.8 4.4 fusion.142
  51.2 30.8 %all-gather.29.cloned.1.call-done = f32[2,512,512]{2,1,0:T(8,128)} async-done(((f32[2,128,512]{2,1,0:T(8,128)}), f32[2,512,512]{2,1,0:T(8,128)}) %all-gather.29.cloned.1.call-update) | async-done | bytes 2097168 | tf_op jit(solution)/shard_map/all_gather | solution.py:47
  82.0 4.4 fusion.147
  86.5 14.2 %all-gather.31.cloned.1.call-done = f32[1024,512]{1,0:T(8,128)} async-done(((f32[512,512]{1,0:T(8,128)}), f32[1024,512]{1,0:T(8,128)}) %all-gather.31.cloned.1.call-update) | async-done | bytes 2097168 | tf_op jit(solution)/shard_map/all_gather | solution.py:21
  102.9 4.4 fusion.136
  107.4 12.2 %all-gather.37.cloned.1.call-done = f32[1024,512]{1,0:T(8,128)} async-done(((f32[512,512]{1,0:T(8,128)}), f32[1024,512]{1,0:T(8,128)}) %all-gather.37.cloned.1.call-update) | async-done | bytes 2097168 | tf_op jit(solution)/shard_map/all_gather | solution.py:21
  121.8 4.4 fusion.84
  126.4 46.0 %all-gather.33.cloned.1.call-done = f32[2048,512]{1,0:T(8,128)} async-done(((f32[512,512]{1,0:T(8,128)}), f32[2048,512]{1,0:T(8,128)}) %all-gather.33.cloned.1.call-update) | async-done | bytes 4194320 | tf_op jit(solution)/shard_map/all_gather | solution.py:21
  175.8 3.1 fusion.121
  182.7 2.8 fusion.129
  186.0 8.1 %all_gather.91 = f32[2,512]{1,0:T(2,128)S(1)} all-gather(f32[2,128]{1,0:T(2,128)S(1)} %bitcast.347), channel_id=1, replica_groups=mesh['tm_0'=8,'tm_1'=4,'tm_2'=2,'blk'=4] {'blk'}, dimensions={1}, use_global_device_ids=true | all-gather | bytes 5120 | tf_op jit(solution)/shard_map/all_gather | solution.py:48
  198.5 4.2 all-gather.12
  203.6 21.6 %all-gather.39.cloned.1.call-done = f32[2048,512]{1,0:T(8,128)} async-done(((f32[512,512]{1,0:T(8,128)}), f32[2048,512]{1,0:T(8,128)}) %all-gather.39.cloned.1.call-update) | async-done | bytes 4194320 | tf_op jit(solution)/shard_map/all_gather | solution.py:21
  228.5 3.1 fusion.69
  235.5 2.8 fusion.77
  238.4 2.5 fusion.134
  243.2 9.4 %all-gather.13 = f32[4,1,512]{2,1,0:T(1,128)S(1)} all-gather(f32[1,1,512]{2,1,0:T(1,128)S(1)} %bitcast.331), channel_id=6, replica_groups=mesh['tm_0'=8,'tm_1'=4,'tm_2'=2,'blk'=4] {'tm_1'}, dimensions={0}, use_global_device_ids=true | all-gather | bytes 10240 | tf_op jit(solution)/shard_map/all_gather | solution.py:21
  261.7 22.3 %all-gather.14 = f32[8,1,512]{2,1,0:T(1,128)S(1)} all-gather(f32[1,1,512]{2,1,0:T(1,128)S(1)} %bitcast.342), channel_id=7, replica_groups=mesh['tm_0'=8,'tm_1'=4,'tm_2'=2,'blk'=4] {'tm_0'}, dimensions={0}, use_global_device_ids=true | all-gather | bytes 18432 | tf_op jit(solution)/shard_map/all_gather | solution.py:21
  284.0 2.4 fusion.67
  287.4 3.0 fusion.6
  290.4 3.0 fusion.20
  293.4 28.4 %all-gather.35.cloned.1.call-done = f32[4096,512]{1,0:T(8,128)} async-done(((f32[512,512]{1,0:T(8,128)}), f32[4096,512]{1,0:T(8,128)}) %all-gather.35.cloned.1.call-update) | async-done | bytes 8388624 | tf_op jit(solution)/shard_map/all_gather | solution.py:21
  324.1 2.3 fusion.93
  326.5 2.5 fusion.97
  361.3 8.5 %all_gather.105 = f32[2,512]{1,0:T(2,128)S(1)} all-gather(f32[2,128]{1,0:T(2,128)S(1)} %bitcast.346), channel_id=1, replica_groups=mesh['tm_0'=8,'tm_1'=4,'tm_2'=2,'blk'=4] {'blk'}, dimensions={1}, use_global_device_ids=true | all-gather | bytes 5120 | tf_op jit(solution)/shard_map/all_gather | solution.py:68
  370.8 3.6 all-gather.15
  375.4 9.5 %all-gather.16 = f32[4,1,512]{2,1,0:T(1,128)S(1)} all-gather(f32[1,1,512]{2,1,0:T(1,128)S(1)} %bitcast.330), channel_id=12, replica_groups=mesh['tm_0'=8,'tm_1'=4,'tm_2'=2,'blk'=4] {'tm_1'}, dimensions={0}, use_global_device_ids=true | all-gather | bytes 10240 | tf_op jit(solution)/shard_map/all_gather | solution.py:21
  387.9 19.5 %all-gather.17 = f32[8,1,512]{2,1,0:T(1,128)S(1)} all-gather(f32[1,1,512]{2,1,0:T(1,128)S(1)} %bitcast.339), channel_id=13, replica_groups=mesh['tm_0'=8,'tm_1'=4,'tm_2'=2,'blk'=4] {'tm_0'}, dimensions={0}, use_global_device_ids=true | all-gather | bytes 18432 | tf_op jit(solution)/shard_map/all_gather | solution.py:21
  408.7 7.8 %all-gather.41.cloned.1.call-done = f32[4096,512]{1,0:T(8,128)} async-done(((f32[512,512]{1,0:T(8,128)}), f32[4096,512]{1,0:T(8,128)}) %all-gather.41.cloned.1.call-update) | async-done | bytes 8388624 | tf_op jit(solution)/shard_map/all_gather | solution.py:21
  418.8 2.3 fusion.41
  421.2 2.5 fusion.45
  (206 shorter events, 113.7 us)
Async XLA Ops:
  7.2 353.7 %copy-start = (f32[2,128,512]{2,1,0:T(8,128)S(1)}, f32[2,128,512]{2,1,0:T(8,128)}, u32[]{:S(2)}) copy-start(f32[2,128,512]{2,1,0:T(8,128)} %param.11) | copy-start | bytes 1572868
  7.2 39.6 %all-gather.27.cloned.1.call-start = ((), (), s32[]{:S(2)}) async-start(), calls=%async_computation | async-start | bytes 2621440 | tf_op jit(solution)/shard_map/all_gather | solution.py:46
  7.9 74.1 %all-gather.29.cloned.1.call-start = ((), (), s32[]{:S(2)}) async-start(), calls=%async_computation.1 | async-start | bytes 2621440 | tf_op jit(solution)/shard_map/all_gather | solution.py:47
  8.7 92.0 %all-gather.31.cloned.1.call-start = ((), (), s32[]{:S(2)}) async-start(), calls=%async_computation.2 | async-start | bytes 3145728 | tf_op jit(solution)/shard_map/all_gather | solution.py:21
  51.2 68.4 %all-gather.37.cloned.1.call-start = ((), (), s32[]{:S(2)}) async-start(), calls=%async_computation.5 | async-start | bytes 3145728 | tf_op jit(solution)/shard_map/all_gather | solution.py:21
  86.4 86.0 %all-gather.33.cloned.1.call-start = ((), (), s32[]{:S(2)}) async-start(), calls=%async_computation.3 | async-start | bytes 5242880 | tf_op jit(solution)/shard_map/all_gather | solution.py:21
  102.9 23.3 %copy-start.13 = (f32[512,512]{1,0:T(8,128)}, f32[512,512]{1,0:T(8,128)S(1)}, u32[]{:S(2)}) copy-start(f32[512,512]{1,0:T(8,128)S(1)} %fusion.35) | copy-start | bytes 3145732
  107.3 117.9 %all-gather.39.cloned.1.call-start = ((), (), s32[]{:S(2)}) async-start(), calls=%async_computation.6 | async-start | bytes 5242880 | tf_op jit(solution)/shard_map/all_gather | solution.py:21
  121.8 53.0 %copy-start.16 = (f32[512,512]{1,0:T(8,128)}, f32[512,512]{1,0:T(8,128)S(1)}, u32[]{:S(2)}) copy-start(f32[512,512]{1,0:T(8,128)S(1)} %fusion.31) | copy-start | bytes 3145732
  126.2 195.6 %all-gather.35.cloned.1.call-start = ((), (), s32[]{:S(2)}) async-start(), calls=%async_computation.4 | async-start | bytes 9437184 | tf_op jit(solution)/shard_map/all_gather | solution.py:21
  172.4 7.4 %copy-start.7 = (f32[2048,512]{1,0:T(8,128)S(1)}, f32[2048,512]{1,0:T(8,128)}, u32[]{:S(2)}) copy-start(f32[2048,512]{1,0:T(8,128)} %all-gather.33.cloned.1.call-done) | copy-start | bytes 12582916
  179.8 22.9 %copy-start.3 = (f32[2,512,512]{2,1,0:T(8,128)S(1)}, f32[2,512,512]{2,1,0:T(8,128)}, u32[]{:S(2)}) copy-start(f32[2,512,512]{2,1,0:T(8,128)} %all-gather.29.cloned.1.call-done) | copy-start | bytes 6291460
  185.6 231.0 %all-gather.41.cloned.1.call-start = ((), (), s32[]{:S(2)}) async-start(), calls=%async_computation.7 | async-start | bytes 9437184 | tf_op jit(solution)/shard_map/all_gather | solution.py:21
  225.2 7.4 %copy-start.5 = (f32[2048,512]{1,0:T(8,128)S(1)}, f32[2048,512]{1,0:T(8,128)}, u32[]{:S(2)}) copy-start(f32[2048,512]{1,0:T(8,128)} %all-gather.39.cloned.1.call-done) | copy-start | bytes 12582916
  238.3 16.9 %copy-start.14 = (f32[512,512]{1,0:T(8,128)S(1)}, f32[512,512]{1,0:T(8,128)}, u32[]{:S(2)}) copy-start(f32[512,512]{1,0:T(8,128)} %copy-done.13) | copy-start | bytes 3145732
  238.3 16.9 %copy-start.15 = (f32[512,512]{1,0:T(8,128)S(1)}, f32[512,512]{1,0:T(8,128)}, u32[]{:S(2)}) copy-start(f32[512,512]{1,0:T(8,128)} %fusion.136) | copy-start | bytes 3145732
  238.3 18.1 %copy-start.17 = (f32[512,512]{1,0:T(8,128)S(1)}, f32[512,512]{1,0:T(8,128)}, u32[]{:S(2)}) copy-start(f32[512,512]{1,0:T(8,128)} %copy-done.16) | copy-start | bytes 3145732
  238.3 18.1 %copy-start.18 = (f32[512,512]{1,0:T(8,128)S(1)}, f32[512,512]{1,0:T(8,128)}, u32[]{:S(2)}) copy-start(f32[512,512]{1,0:T(8,128)} %fusion.84) | copy-start | bytes 3145732
  240.8 16.8 %copy-start.8 = (f32[2048,512]{1,0:T(8,128)S(1)}, f32[2048,512]{1,0:T(8,128)}, u32[]{:S(2)}) copy-start(f32[2048,512]{1,0:T(8,128)} %all-gather.33.cloned.1.call-done) | copy-start | bytes 12582916
  256.4 31.0 %copy-start.10 = (f32[512,512]{1,0:T(8,128)S(1)}, f32[512,512]{1,0:T(8,128)}, u32[]{:S(2)}) copy-start(f32[512,512]{1,0:T(8,128)} %copy-done.9) | copy-start | bytes 3145732
  256.4 31.0 %copy-start.12 = (f32[512,512]{1,0:T(8,128)S(1)}, f32[512,512]{1,0:T(8,128)}, u32[]{:S(2)}) copy-start(f32[512,512]{1,0:T(8,128)} %copy-done.11) | copy-start | bytes 3145732
  256.4 31.0 %copy-start.25 = (f32[512,512]{1,0:T(8,128)S(1)}, f32[512,512]{1,0:T(8,128)}, u32[]{:S(2)}) copy-start(f32[512,512]{1,0:T(8,128)} %fusion.129) | copy-start | bytes 3145732
  256.4 31.0 %copy-start.27 = (f32[512,512]{1,0:T(8,128)S(1)}, f32[512,512]{1,0:T(8,128)}, u32[]{:S(2)}) copy-start(f32[512,512]{1,0:T(8,128)} %copy-done.26) | copy-start | bytes 3145732
  257.6 32.8 %copy-start.31 = (f32[512,512]{1,0:T(8,128)}, f32[512,512]{1,0:T(8,128)S(1)}, u32[]{:S(2)}) copy-start(f32[512,512]{1,0:T(8,128)S(1)} %fusion.15) | copy-start | bytes 3145732
  284.0 6.4 %copy-start.22 = (f32[512,512]{1,0:T(8,128)S(1)}, f32[512,512]{1,0:T(8,128)}, u32[]{:S(2)}) copy-start(f32[512,512]{1,0:T(8,128)} %copy-done.21) | copy-start | bytes 3145732
  321.8 18.5 %copy-start.30 = (f32[512,512]{1,0:T(8,128)S(1)}, f32[512,512]{1,0:T(8,128)}, u32[]{:S(2)}) copy-start(f32[512,512]{1,0:T(8,128)} %fusion.6) | copy-start | bytes 3145732
  324.1 17.1 %copy-start.2 = (f32[4096,512]{1,0:T(8,128)S(1)}, f32[4096,512]{1,0:T(8,128)}, u32[]{:S(2)}) copy-start(f32[4096,512]{1,0:T(8,128)} %all-gather.35.cloned.1.call-done) | copy-start | bytes 25165828
  353.6 20.8 %copy-start.33 = (f32[1024,512]{1,0:T(8,128)S(1)}, f32[1024,512]{1,0:T(8,128)}, u32[]{:S(2)}) copy-start(f32[1024,512]{1,0:T(8,128)} %all-gather.37.cloned.1.call-done) | copy-start | bytes 6291460
  355.9 28.9 %copy-start.6 = (f32[2048,512]{1,0:T(8,128)S(1)}, f32[2048,512]{1,0:T(8,128)}, u32[]{:S(2)}) copy-start(f32[2048,512]{1,0:T(8,128)} %all-gather.39.cloned.1.call-done) | copy-start | bytes 12582916
  358.8 48.9 %copy-start.32 = (f32[512,512]{1,0:T(8,128)S(1)}, f32[512,512]{1,0:T(8,128)}, u32[]{:S(2)}) copy-start(f32[512,512]{1,0:T(8,128)} %copy-done.31) | copy-start | bytes 3145732
  416.5 18.3 %copy-start.24 = (f32[512,512]{1,0:T(8,128)S(1)}, f32[512,512]{1,0:T(8,128)}, u32[]{:S(2)}) copy-start(f32[512,512]{1,0:T(8,128)} %fusion.20) | copy-start | bytes 3145732
  418.8 17.0 %copy-start.1 = (f32[4096,512]{1,0:T(8,128)S(1)}, f32[4096,512]{1,0:T(8,128)}, u32[]{:S(2)}) copy-start(f32[4096,512]{1,0:T(8,128)} %all-gather.41.cloned.1.call-done) | copy-start | bytes 25165828
  (14 other events, 48.1 us)
Sparse Core Ops, SparseCore 0:
  9.8 36.9 all-gather.26
  48.6 33.3 all-gather.28
  83.8 16.8 all-gather.30
  102.3 17.1 all-gather.36
  121.2 51.1 all-gather.32
  174.1 51.0 all-gather.38
  227.0 94.7 all-gather.34
  323.6 92.9 all-gather.40
where the time goes:
time: 471 us; the launch traced here: 463 us
  waiting for transfers between devices  200 us (42%)
  matrix products  155 us (33%)
  blocking collectives  85.1 us (18%)
  between operations  15.1 us (3%)
  local copies, waits for them, and re-layouts  6.15 us (1%)
    all_gather x6, waiting for transfers between devices, prefix_by_axis(): pieces = jax.tree.map(lambda part: lax.all_gather(part, axis), so_far)  130 us
    dot_general x34, matrix products, chain_combine(): joined_map = jnp.dot(later[0], earlier[0], precision=highest)  74.4 us
    all_gather x6, blocking collectives, prefix_by_axis(): pieces = jax.tree.map(lambda part: lax.all_gather(part, axis), so_far)  68.5 us
    dot_general x34, matrix products, chain_combine(): joined_offset = jnp.dot(later[0], earlier[1], precision=highest) + later[1]  58.5 us
    all_gather x1, waiting for transfers between devices, shards(): lax.all_gather(filter_map, 'blk', axis=1, tiled=True)  38.1 us
    all_gather x1, waiting for transfers between devices, shards(): lax.all_gather(smoother_gain, 'blk', axis=1, tiled=True)  30.8 us
  transfers between devices with their start and end apart: 8, of which 8 were waited for; matrix products, arithmetic and copies ran while one was open for 25% of the time, Pallas kernels for 0%

commit v1 on v0

--- a/solution.py
+++ b/solution.py
@@ -43,7 +43,9 @@
     first_row = lax.axis_index("blk") * rows
     drive_rows = jnp.einsum("tro,to->tr", obs_gain, observations, precision=highest)
     full_filter, full_gain, drive = (
-        lax.all_gather(filter_map, "blk", axis=1, tiled=True),
+        jnp.concatenate(
+            lax.all_to_all(jnp.stack([filter_map] * lax.axis_size("blk")), "blk", 0, 0), axis=1
+        ),
         lax.all_gather(smoother_gain, "blk", axis=1, tiled=True),
         lax.all_gather(drive_rows, "blk", axis=1, tiled=True),
     )

time: 471 us -> 448 us (0.951)
  waiting for transfers between devices: 200 us -> 140 us
  blocking collectives: 85.1 us -> 125 us
  matrix products: 155 us -> 149 us
    all_to_all x0 -> x1, blocking collectives: none -> 39.5 us  [shards(): lax.all_to_all(jnp.stack([filter_map] * lax.axis_size('blk')), 'blk', 0, 0)]
    all_gather x1 -> x0, waiting for transfers between devices: 38.1 us -> none  [shards(): lax.all_gather(filter_map, 'blk', axis=1, tiled=True)]
    all_gather x1, waiting for transfers between devices: 30.8 us -> 5.87 us  [shards(): lax.all_gather(smoother_gain, 'blk', axis=1, tiled=True)]
  transfers between devices with their start and end apart: 8 -> 7, of which waited for: 8 -> 7; matrix products, arithmetic and copies ran while one was open for 25% -> 26% of each run, Pallas kernels for 0% -> 0%
where the time goes in v1:
time: 448 us; the launch traced here: 439 us
  matrix products  149 us (33%)
  waiting for transfers between devices  140 us (31%)
  blocking collectives  125 us (28%)
  between operations  15.2 us (3%)
  local copies, waits for them, and re-layouts  9.67 us (2%)
    all_gather x6, waiting for transfers between devices, prefix_by_axis(): pieces = jax.tree.map(lambda part: lax.all_gather(part, axis), so_far)  133 us
    dot_general x34, matrix products, chain_combine(): joined_map = jnp.dot(later[0], earlier[0], precision=highest)  73.7 us
    all_gather x6, blocking collectives, prefix_by_axis(): pieces = jax.tree.map(lambda part: lax.all_gather(part, axis), so_far)  68.5 us
    dot_general x34, matrix products, chain_combine(): joined_offset = jnp.dot(later[0], earlier[1], precision=highest) + later[1]  57.7 us
    all_to_all x1, blocking collectives, shards(): lax.all_to_all(jnp.stack([filter_map] * lax.axis_size('blk')), 'blk', 0, 0)  39.5 us
  transfers between devices with their start and end apart: 7, of which 7 were waited for; matrix products, arithmetic and copies ran while one was open for 26% of the time, Pallas kernels for 0%

profile of v1, /device:TPU:1, one launch (start us, length us, event | category | flops | bytes accessed | tf_op | source)
XLA Modules:
  0.0 439.4 jit_solution(847145064382921883)
XLA Ops:
  9.3 39.5 %all_to_all.5 = f32[4,2,128,512]{3,2,1,0:T(8,128)S(1)} all-to-all(f32[4,2,128,512]{3,2,1,0:T(8,128)S(1)} %stack.25), channel_id=1, replica_groups=mesh['tm_0'=8,'tm_1'=4,'tm_2'=2,'blk'=4] {'blk'}, dimensions={0} | all-to-all | bytes 4194304 | tf_op jit(solution)/shard_map/all_to_all | solution.py:47
  48.9 2.9 fusion.188
  51.9 5.9 %all-gather.26.cloned.1.call-done = f32[2,512,512]{2,1,0:T(8,128)} async-done(((f32[2,128,512]{2,1,0:T(8,128)}), f32[2,512,512]{2,1,0:T(8,128)}) %all-gather.26.cloned.1.call-update) | async-done | bytes 2097168 | tf_op jit(solution)/shard_map/all_gather | solution.py:49
  57.7 4.4 fusion.142
  62.2 15.1 %all-gather.28.cloned.1.call-done = f32[1024,512]{1,0:T(8,128)} async-done(((f32[512,512]{1,0:T(8,128)}), f32[1024,512]{1,0:T(8,128)}) %all-gather.28.cloned.1.call-update) | async-done | bytes 2097168 | tf_op jit(solution)/shard_map/all_gather | solution.py:21
  80.5 4.0 fusion.136
  84.6 11.8 %all-gather.34.cloned.1.call-done = f32[1024,512]{1,0:T(8,128)} async-done(((f32[512,512]{1,0:T(8,128)}), f32[1024,512]{1,0:T(8,128)}) %all-gather.34.cloned.1.call-update) | async-done | bytes 2097168 | tf_op jit(solution)/shard_map/all_gather | solution.py:21
  99.5 4.1 fusion.84
  103.8 45.3 %all-gather.30.cloned.1.call-done = f32[2048,512]{1,0:T(8,128)} async-done(((f32[512,512]{1,0:T(8,128)}), f32[2048,512]{1,0:T(8,128)}) %all-gather.30.cloned.1.call-update) | async-done | bytes 4194320 | tf_op jit(solution)/shard_map/all_gather | solution.py:21
  152.5 3.1 fusion.121
  159.5 2.8 fusion.129
  162.8 8.1 %all_gather.87 = f32[2,512]{1,0:T(2,128)S(1)} all-gather(f32[2,128]{1,0:T(2,128)S(1)} %bitcast.353), channel_id=1, replica_groups=mesh['tm_0'=8,'tm_1'=4,'tm_2'=2,'blk'=4] {'blk'}, dimensions={1}, use_global_device_ids=true | all-gather | bytes 5120 | tf_op jit(solution)/shard_map/all_gather | solution.py:50
  172.8 4.2 all-gather.12
  177.0 25.0 %all-gather.36.cloned.1.call-done = f32[2048,512]{1,0:T(8,128)} async-done(((f32[512,512]{1,0:T(8,128)}), f32[2048,512]{1,0:T(8,128)}) %all-gather.36.cloned.1.call-update) | async-done | bytes 4194320 | tf_op jit(solution)/shard_map/all_gather | solution.py:21
  205.3 3.1 fusion.69
  212.2 2.9 fusion.77
  216.1 3.0 fusion.134
  219.1 2.3 fusion.138
  221.5 9.4 %all-gather.13 = f32[4,1,512]{2,1,0:T(1,128)S(1)} all-gather(f32[1,1,512]{2,1,0:T(1,128)S(1)} %bitcast.338), channel_id=6, replica_groups=mesh['tm_0'=8,'tm_1'=4,'tm_2'=2,'blk'=4] {'tm_1'}, dimensions={0}, use_global_device_ids=true | all-gather | bytes 10240 | tf_op jit(solution)/shard_map/all_gather | solution.py:21
  238.7 22.4 %all-gather.14 = f32[8,1,512]{2,1,0:T(1,128)S(1)} all-gather(f32[1,1,512]{2,1,0:T(1,128)S(1)} %bitcast.348), channel_id=7, replica_groups=mesh['tm_0'=8,'tm_1'=4,'tm_2'=2,'blk'=4] {'tm_0'}, dimensions={0}, use_global_device_ids=true | all-gather | bytes 18432 | tf_op jit(solution)/shard_map/all_gather | solution.py:21
  262.1 3.0 fusion.6
  267.4 3.0 fusion.20
  270.4 28.0 %all-gather.32.cloned.1.call-done = f32[4096,512]{1,0:T(8,128)} async-done(((f32[512,512]{1,0:T(8,128)}), f32[4096,512]{1,0:T(8,128)}) %all-gather.32.cloned.1.call-update) | async-done | bytes 8388624 | tf_op jit(solution)/shard_map/all_gather | solution.py:21
  300.7 2.3 fusion.93
  303.1 2.5 fusion.97
  338.0 8.5 %all_gather.101 = f32[2,512]{1,0:T(2,128)S(1)} all-gather(f32[2,128]{1,0:T(2,128)S(1)} %bitcast.352), channel_id=1, replica_groups=mesh['tm_0'=8,'tm_1'=4,'tm_2'=2,'blk'=4] {'blk'}, dimensions={1}, use_global_device_ids=true | all-gather | bytes 5120 | tf_op jit(solution)/shard_map/all_gather | solution.py:70
  347.5 3.6 all-gather.15
  352.0 9.5 %all-gather.16 = f32[4,1,512]{2,1,0:T(1,128)S(1)} all-gather(f32[1,1,512]{2,1,0:T(1,128)S(1)} %bitcast.337), channel_id=12, replica_groups=mesh['tm_0'=8,'tm_1'=4,'tm_2'=2,'blk'=4] {'tm_1'}, dimensions={0}, use_global_device_ids=true | all-gather | bytes 10240 | tf_op jit(solution)/shard_map/all_gather | solution.py:21
  364.5 19.5 %all-gather.17 = f32[8,1,512]{2,1,0:T(1,128)S(1)} all-gather(f32[1,1,512]{2,1,0:T(1,128)S(1)} %bitcast.346), channel_id=13, replica_groups=mesh['tm_0'=8,'tm_1'=4,'tm_2'=2,'blk'=4] {'tm_0'}, dimensions={0}, use_global_device_ids=true | all-gather | bytes 18432 | tf_op jit(solution)/shard_map/all_gather | solution.py:21
  385.4 7.8 %all-gather.38.cloned.1.call-done = f32[4096,512]{1,0:T(8,128)} async-done(((f32[512,512]{1,0:T(8,128)}), f32[4096,512]{1,0:T(8,128)}) %all-gather.38.cloned.1.call-update) | async-done | bytes 8388624 | tf_op jit(solution)/shard_map/all_gather | solution.py:21
  395.4 2.3 fusion.41
  397.8 2.5 fusion.45
  (214 shorter events, 112.7 us)
Async XLA Ops:
  7.2 330.3 %copy-start = (f32[2,128,512]{2,1,0:T(8,128)S(1)}, f32[2,128,512]{2,1,0:T(8,128)}, u32[]{:S(2)}) copy-start(f32[2,128,512]{2,1,0:T(8,128)} %param.11) | copy-start | bytes 1572868
  7.2 50.5 %all-gather.26.cloned.1.call-start = ((), (), s32[]{:S(2)}) async-start(), calls=%async_computation.1 | async-start | bytes 2621440 | tf_op jit(solution)/shard_map/all_gather | solution.py:49
  7.9 69.4 %all-gather.28.cloned.1.call-start = ((), (), s32[]{:S(2)}) async-start(), calls=%async_computation.2 | async-start | bytes 3145728 | tf_op jit(solution)/shard_map/all_gather | solution.py:21
  48.9 122.0 %copy-start.10 = (f32[1,4,128,512]{3,2,0,1:T(8,128)}, f32[1,4,128,512]{3,2,0,1:T(8,128)S(1)}, u32[]{:S(2)}) copy-start(f32[1,4,128,512]{3,2,0,1:T(8,128)S(1)} %get-tuple-element.10) | copy-start | bytes 3145732
  48.9 122.9 %copy-start.8 = (f32[1,4,128,512]{3,2,0,1:T(8,128)}, f32[1,4,128,512]{3,2,0,1:T(8,128)S(1)}, u32[]{:S(2)}) copy-start(f32[1,4,128,512]{3,2,0,1:T(8,128)S(1)} %get-tuple-element.11) | copy-start | bytes 3145732
  51.8 44.5 %all-gather.34.cloned.1.call-start = ((), (), s32[]{:S(2)}) async-start(), calls=%async_computation.5 | async-start | bytes 3145728 | tf_op jit(solution)/shard_map/all_gather | solution.py:21
  62.1 87.0 %all-gather.30.cloned.1.call-start = ((), (), s32[]{:S(2)}) async-start(), calls=%async_computation.3 | async-start | bytes 5242880 | tf_op jit(solution)/shard_map/all_gather | solution.py:21
  84.5 117.4 %all-gather.36.cloned.1.call-start = ((), (), s32[]{:S(2)}) async-start(), calls=%async_computation.6 | async-start | bytes 5242880 | tf_op jit(solution)/shard_map/all_gather | solution.py:21
  103.6 194.8 %all-gather.32.cloned.1.call-start = ((), (), s32[]{:S(2)}) async-start(), calls=%async_computation.4 | async-start | bytes 9437184 | tf_op jit(solution)/shard_map/all_gather | solution.py:21
  149.2 7.4 %copy-start.6 = (f32[2048,512]{1,0:T(8,128)S(1)}, f32[2048,512]{1,0:T(8,128)}, u32[]{:S(2)}) copy-start(f32[2048,512]{1,0:T(8,128)} %all-gather.30.cloned.1.call-done) | copy-start | bytes 12582916
  162.3 230.8 %all-gather.38.cloned.1.call-start = ((), (), s32[]{:S(2)}) async-start(), calls=%async_computation.7 | async-start | bytes 9437184 | tf_op jit(solution)/shard_map/all_gather | solution.py:21
  201.9 7.4 %copy-start.4 = (f32[2048,512]{1,0:T(8,128)S(1)}, f32[2048,512]{1,0:T(8,128)}, u32[]{:S(2)}) copy-start(f32[2048,512]{1,0:T(8,128)} %all-gather.36.cloned.1.call-done) | copy-start | bytes 12582916
  215.1 16.2 %copy-start.17 = (f32[512,512]{1,0:T(8,128)S(1)}, f32[512,512]{1,0:T(8,128)}, u32[]{:S(2)}) copy-start(f32[512,512]{1,0:T(8,128)} %copy-done.16) | copy-start | bytes 3145732
  215.1 16.2 %copy-start.18 = (f32[512,512]{1,0:T(8,128)S(1)}, f32[512,512]{1,0:T(8,128)}, u32[]{:S(2)}) copy-start(f32[512,512]{1,0:T(8,128)} %fusion.136) | copy-start | bytes 3145732
  215.1 17.3 %copy-start.36 = (f32[1024,512]{1,0:T(8,128)S(1)}, f32[1024,512]{1,0:T(8,128)}, u32[]{:S(2)}) copy-start(f32[1024,512]{1,0:T(8,128)} %all-gather.34.cloned.1.call-done) | copy-start | bytes 6291460
  215.1 18.3 %copy-start.20 = (f32[512,512]{1,0:T(8,128)S(1)}, f32[512,512]{1,0:T(8,128)}, u32[]{:S(2)}) copy-start(f32[512,512]{1,0:T(8,128)} %copy-done.19) | copy-start | bytes 3145732
  215.1 18.3 %copy-start.21 = (f32[512,512]{1,0:T(8,128)S(1)}, f32[512,512]{1,0:T(8,128)}, u32[]{:S(2)}) copy-start(f32[512,512]{1,0:T(8,128)} %fusion.84) | copy-start | bytes 3145732
  219.1 15.6 %copy-start.7 = (f32[2048,512]{1,0:T(8,128)S(1)}, f32[2048,512]{1,0:T(8,128)}, u32[]{:S(2)}) copy-start(f32[2048,512]{1,0:T(8,128)} %all-gather.30.cloned.1.call-done) | copy-start | bytes 12582916
  233.4 28.7 %copy-start.13 = (f32[512,512]{1,0:T(8,128)S(1)}, f32[512,512]{1,0:T(8,128)}, u32[]{:S(2)}) copy-start(f32[512,512]{1,0:T(8,128)} %copy-done.12) | copy-start | bytes 3145732
  233.5 28.7 %copy-start.15 = (f32[512,512]{1,0:T(8,128)S(1)}, f32[512,512]{1,0:T(8,128)}, u32[]{:S(2)}) copy-start(f32[512,512]{1,0:T(8,128)} %copy-done.14) | copy-start | bytes 3145732
  233.5 28.7 %copy-start.28 = (f32[512,512]{1,0:T(8,128)S(1)}, f32[512,512]{1,0:T(8,128)}, u32[]{:S(2)}) copy-start(f32[512,512]{1,0:T(8,128)} %fusion.129) | copy-start | bytes 3145732
  233.5 28.7 %copy-start.30 = (f32[512,512]{1,0:T(8,128)S(1)}, f32[512,512]{1,0:T(8,128)}, u32[]{:S(2)}) copy-start(f32[512,512]{1,0:T(8,128)} %copy-done.29) | copy-start | bytes 3145732
  234.7 32.7 %copy-start.34 = (f32[512,512]{1,0:T(8,128)}, f32[512,512]{1,0:T(8,128)S(1)}, u32[]{:S(2)}) copy-start(f32[512,512]{1,0:T(8,128)S(1)} %fusion.15) | copy-start | bytes 3145732
  261.1 6.3 %copy-start.26 = (f32[512,512]{1,0:T(8,128)S(1)}, f32[512,512]{1,0:T(8,128)}, u32[]{:S(2)}) copy-start(f32[512,512]{1,0:T(8,128)} %fusion.77) | copy-start | bytes 3145732
  261.1 6.3 %copy-start.32 = (f32[512,512]{1,0:T(8,128)S(1)}, f32[512,512]{1,0:T(8,128)}, u32[]{:S(2)}) copy-start(f32[512,512]{1,0:T(8,128)} %copy-done.31) | copy-start | bytes 3145732
  298.4 18.5 %copy-start.33 = (f32[512,512]{1,0:T(8,128)S(1)}, f32[512,512]{1,0:T(8,128)}, u32[]{:S(2)}) copy-start(f32[512,512]{1,0:T(8,128)} %fusion.6) | copy-start | bytes 3145732
  300.7 17.1 %copy-start.2 = (f32[4096,512]{1,0:T(8,128)S(1)}, f32[4096,512]{1,0:T(8,128)}, u32[]{:S(2)}) copy-start(f32[4096,512]{1,0:T(8,128)} %all-gather.32.cloned.1.call-done) | copy-start | bytes 25165828
  332.6 18.5 %copy-start.37 = (f32[1024,512]{1,0:T(8,128)S(1)}, f32[1024,512]{1,0:T(8,128)}, u32[]{:S(2)}) copy-start(f32[1024,512]{1,0:T(8,128)} %all-gather.34.cloned.1.call-done) | copy-start | bytes 6291460
  332.6 29.0 %copy-start.5 = (f32[2048,512]{1,0:T(8,128)S(1)}, f32[2048,512]{1,0:T(8,128)}, u32[]{:S(2)}) copy-start(f32[2048,512]{1,0:T(8,128)} %all-gather.36.cloned.1.call-done) | copy-start | bytes 12582916
  335.5 48.9 %copy-start.35 = (f32[512,512]{1,0:T(8,128)S(1)}, f32[512,512]{1,0:T(8,128)}, u32[]{:S(2)}) copy-start(f32[512,512]{1,0:T(8,128)} %copy-done.34) | copy-start | bytes 3145732
  393.1 18.3 %copy-start.27 = (f32[512,512]{1,0:T(8,128)S(1)}, f32[512,512]{1,0:T(8,128)}, u32[]{:S(2)}) copy-start(f32[512,512]{1,0:T(8,128)} %fusion.20) | copy-start | bytes 3145732
  395.4 17.0 %copy-start.1 = (f32[4096,512]{1,0:T(8,128)S(1)}, f32[4096,512]{1,0:T(8,128)}, u32[]{:S(2)}) copy-start(f32[4096,512]{1,0:T(8,128)} %all-gather.38.cloned.1.call-done) | copy-start | bytes 25165828
  (17 other events, 55.4 us)
Sparse Core Ops, SparseCore 0:
  9.8 47.8 all-gather.25
  59.5 17.7 all-gather.27
  79.1 17.1 all-gather.33
  98.0 51.1 all-gather.29
  150.8 51.0 all-gather.35
  203.6 94.7 all-gather.31
  300.2 92.9 all-gather.37
